TPU v7x, 32 devices: a whole 2x2x4 slice. The times are simulated.
32 devices in a mesh: groups: 2 (over y), ep: 4 (over z), tok: 4 (over x, core).
Axes of the slice: x: 2, y: 2, z: 4, core: 2. Of those that a mesh axis runs over, the one named last changes fastest.
Arguments:
- tokens: bfloat16 [128, 7168], P(('groups', 'ep', 'tok')), parts along dimension 0, may hold values from -6 to 6
- expert_ids: int32 [128, 2], P(('groups', 'ep', 'tok')), parts along dimension 0, may hold values from 0 to 3, all different within a row; in each aligned block of 4 rows (0 to 3, 4 to 7, ...) at most 3 rows name the same one
- gate_fixed: int32 [128, 2], P(('groups', 'ep', 'tok')), parts along dimension 0, may hold values from 1 to 65535
- w_gate: bfloat16 [4, 7168, 2048], P('ep', None, 'tok'), may hold values from -0.0625 to 0.0625
- w_up: bfloat16 [4, 7168, 2048], P('ep', None, 'tok'), may hold values from -0.0625 to 0.0625
- w_down: bfloat16 [4, 2048, 7168], P('ep', 'tok'), may hold values from -0.125 to 0.125
Outputs:
- layer_out: bfloat16 [128, 7168], P(('groups', 'ep', 'tok')), parts along dimension 0
There are 2 independent parts, one for each index of `groups`. A program takes and returns all parts, laid end to end along the dimension named above; an argument that names none is the same for every part. Nothing has to cross between parts.
Inputs may be any that keep to these rules, and one draw needn't show every extreme that they name: `expert_ids`: each row names 2 different experts. Among the 4 rows of one device no expert is named more than 3 times.
All inputs are finite; a program needn't handle non-finite values.
Results may differ from a plain program's by a relative error of at most 0.014.
Values may be sent and summed in bfloat16 or wider, within the bound.
A program may use at most 64 MiB of HBM per device.

v0:
```python
import jax
import jax.numpy as jnp
from jax import lax
from jax.sharding import PartitionSpec as P


def placing_one(routes, label, capacity):
    tok_dev = routes.shape[0]
    hit_count = jnp.sum((routes == label).astype(jnp.int32), axis=1)
    earlier = (
        lax.broadcasted_iota(jnp.int32, (tok_dev, tok_dev), 1)
        < lax.broadcasted_iota(jnp.int32, (tok_dev, tok_dev), 0)
    ).astype(jnp.int32)
    position = jnp.sum(earlier * hit_count[None, :], axis=1)
    slot_index = lax.broadcasted_iota(jnp.int32, (capacity, tok_dev), 0)
    return ((hit_count[None, :] == 1) & (position[None, :] == slot_index)).astype(jnp.bfloat16)


def per_device(tokens, expert_ids, gate_fixed, w_gate, w_up, w_down):
    tok_dev, model_width = tokens.shape
    columns = lax.axis_size("ep")
    capacity = (3 * tok_dev + 3) // 4
    labels = lax.iota(jnp.int32, columns)
    placing_all = jax.vmap(lambda label: placing_one(expert_ids, label, capacity))(labels)
    outgoing = jnp.einsum(
        "emt,td->emd", placing_all, tokens, preferred_element_type=jnp.float32
    ).astype(jnp.bfloat16)
    slot_rows = lax.all_to_all(outgoing, "ep", split_axis=0, concat_axis=0, tiled=True)
    slot_flat = slot_rows.reshape(columns * capacity, model_width)
    gate_slice = w_gate[0]
    up_slice = w_up[0]
    down_slice = w_down[0]
    segment = lax.all_gather(slot_flat, "tok", axis=0, tiled=True)
    gate = jnp.dot(segment, gate_slice, preferred_element_type=jnp.float32)
    up_val = jnp.dot(segment, up_slice, preferred_element_type=jnp.float32)
    hidden = (jax.nn.silu(gate) * up_val).astype(jnp.bfloat16)
    segment = hidden
    summed = lax.psum_scatter(
        jnp.dot(segment, down_slice, preferred_element_type=jnp.float32).astype(jnp.bfloat16),
        "tok",
        scatter_dimension=0,
        tiled=True,
    ).astype(jnp.float32)
    returned = lax.all_to_all(
        summed.reshape(columns, capacity, model_width).astype(jnp.bfloat16),
        "ep",
        split_axis=0,
        concat_axis=0,
        tiled=True,
    ).astype(jnp.float32)
    scores = gate_fixed.astype(jnp.float32)
    weights = 2.5 * scores / jnp.sum(scores, axis=1, keepdims=True)
    matches = (expert_ids[:, :, None] == labels[None, None, :]).astype(jnp.float32)
    token_expert = jnp.sum(weights[:, :, None] * matches, axis=1)
    placing_f = placing_all.astype(jnp.float32)
    slot_weight = jnp.sum(placing_f * jnp.transpose(token_expert)[:, None, :], axis=2)
    weighted = returned * slot_weight[:, :, None]
    combined = jnp.einsum(
        "emt,emd->td",
        placing_f,
        weighted,
        precision=lax.Precision.HIGHEST,
        preferred_element_type=jnp.float32,
    )
    return combined.astype(jnp.bfloat16)


def solution(mesh):
    in_specs = (
        P(("groups", "ep", "tok"), None),
        P(("groups", "ep", "tok"), None),
        P(("groups", "ep", "tok"), None),
        P("ep", None, "tok"),
        P("ep", None, "tok"),
        P("ep", "tok", None),
    )
    out_specs = P(("groups", "ep", "tok"), None)
    return jax.shard_map(
        per_device, mesh=mesh, in_specs=in_specs, out_specs=out_specs, check_vma=False
    )
```

profile of v0, /device:TPU:1, one launch (start us, length us, event | category | flops | bytes accessed | tf_op | source)
XLA Modules:
  0.0 69.4 jit_solution(11465273859720313877)
XLA Ops:
  0.0 0.0 copy-start
  0.0 0.7 %convert_reduce_fusion = s32[4,4]{1,0:T(4,128)S(1)} fusion(s32[4,2]{0,1:T(2,128)} %param.7), kind=kLoop, calls=%fused_computation.27 | loop fusion | flops 80 | bytes 96 | tf_op jit(solution)/shard_map/vmap()/reduce_sum | solution.py:9
  0.7 0.1 multiply_reduce_fusion
  0.9 0.1 copy.29
  1.0 0.1 copy.28
  1.1 0.0 copy-done
  1.1 0.3 convolution_convert_fusion.1
  1.4 0.1 copy.31
  1.5 11.4 %all_to_all.10 = bf16[4,3,7168]{2,1,0:T(4,128)(2,1)S(1)} all-to-all(bf16[4,3,7168]{2,1,0:T(4,128)(2,1)S(1)} %copy.31), channel_id=1, replica_groups=mesh['groups'=2,'ep'=4,'tok'=4] {'ep'}, dimensions={0} | all-to-all | bytes 344064 | tf_op jit(solution)/shard_map/all_to_all | solution.py:28
  13.0 0.2 reshape.26
  13.1 12.1 %all-gather = bf16[4,12,7168]{2,1,0:T(8,128)(2,1)S(1)} all-gather(bf16[1,12,7168]{2,1,0:T(8,128)(2,1)S(1)} %reshape.26), channel_id=1, replica_groups=mesh['groups'=2,'ep'=4,'tok'=4] {'tok'}, dimensions={0}, use_global_device_ids=true | all-gather | bytes 860160 | tf_op jit(solution)/shard_map/all_gather | solution.py:33
  25.2 0.2 reshape.27
  25.3 4.4 %fusion.5 = f32[48,512]{1,0:T(8,128)S(1)} fusion(bf16[48,7168]{1,0:T(8,128)(2,1)S(1)} %reshape.27, bf16[1,7168,512]{2,1,0:T(8,128)(2,1)} %param.9), kind=kOutput, calls=%fused_computation.7 | convolution fusion | flops 352321536 | bytes 8126464 | tf_op jit(solution)/shard_map/dot_general | solution.py:34
  29.8 0.0 copy-start.3
  29.8 0.0 copy-start.2
  29.8 0.0 copy-start.1
  29.8 7.9 %convolution_convert_fusion = bf16[48,7168]{1,0:T(8,128)(2,1)S(1)} fusion(bf16[1,512,7168]{2,1,0:T(8,128)(2,1)} %param.11, bf16[48,7168]{1,0:T(8,128)(2,1)S(1)} %reshape.27, bf16[1,7168,512]{2,1,0:T(8,128)(2,1)} %param.10, f32[48,512]{1,0:T(8,128)S(1)} %fusion.5), kind=kOutput, calls=%fused_computation | convolution fusion | flops 705134592 | bytes 16154624 | tf_op jit(solution)/shard_map/dot_general | solution.py:39
  37.7 11.4 %fusion = bf16[16,7168]{1,0:T(8,128)(2,1)S(1)} fusion(bf16[48,7168]{1,0:T(8,128)(2,1)S(1)} %convolution_convert_fusion), kind=kCustom, calls=%all-reduce-scatter | all-reduce-scatter fusion | flops 458753 | bytes 918016
  49.2 0.1 slice
  49.2 4.4 %collective-permute-start = (bf16[12,7168]{1,0:T(8,128)(2,1)S(1)}, bf16[12,7168]{1,0:T(8,128)(2,1)S(1)}, u32[]{:S(2)}, u32[]{:S(2)}) collective-permute-start(bf16[12,7168]{1,0:T(8,128)(2,1)S(1)} %slice), channel_id=1, source_target_pairs={{0,1},{1,2},{2,3},{4,5},{5,6},{6,7},{8,9},{9,10},{10,11},{12,13},{... | collective-permute-start | bytes 516104
  53.6 0.0 copy-done.3
  53.6 0.6 dynamic-slice.4
  54.9 0.0 copy-done.2
  54.9 1.7 %collective-permute-done = bf16[12,7168]{1,0:T(8,128)(2,1)S(1)} collective-permute-done((bf16[12,7168]{1,0:T(8,128)(2,1)S(1)}, bf16[12,7168]{1,0:T(8,128)(2,1)S(1)}, u32[]{:S(2)}, u32[]{:S(2)}) %collective-permute-start) | collective-permute-done | bytes 172064
  56.6 0.6 concatenate
  57.2 0.1 constant_dynamic-slice_fusion
  57.3 0.8 %convert_element_type.45 = bf16[4,3,7168]{2,1,0:T(4,128)(2,1)} reshape(bf16[12,7168]{1,0:T(8,128)(2,1)S(1)} %constant_dynamic-slice_fusion) | data formatting | bytes 344064 | tf_op jit(solution)/shard_map/convert_element_type | solution.py:45
  58.1 3.4 %all-to-all-start.1 = ((bf16[4,3,7168]{2,1,0:T(4,128)(2,1)}), bf16[4,3,7168]{2,1,0:T(4,128)(2,1)S(1)}, u32[]{:S(2)}, u32[]{:S(2)}) async-start(bf16[4,3,7168]{2,1,0:T(4,128)(2,1)} %convert_element_type.45), calls=%async_computation.1 | async-start | bytes 458752 | tf_op jit(solution)/shard_map/all_to_all | solution.py:44
  61.5 0.0 copy-done.1
  61.5 0.1 select_reduce_fusion
  61.6 0.1 copy.32
  61.7 6.3 %all-to-all-done.1 = bf16[4,3,7168]{2,1,0:T(4,128)(2,1)S(1)} async-done(((bf16[4,3,7168]{2,1,0:T(4,128)(2,1)}), bf16[4,3,7168]{2,1,0:T(4,128)(2,1)S(1)}, u32[]{:S(2)}, u32[]{:S(2)}) %all-to-all-start.1) | async-done | bytes 172064 | tf_op jit(solution)/shard_map/all_to_all | solution.py:44
  68.0 0.1 convert_multiply_fusion
  68.1 1.3 %fusion.1 = bf16[4,7168]{1,0:T(4,128)(2,1)} fusion(f32[4,3,7168]{2,1,0:T(4,128)S(1)} %convert_multiply_fusion, s32[4,4]{0,1:T(4,128)S(1)} %copy.29, pred[4,4]{0,1:T(4,128)(4,1)S(1)} %copy.28), kind=kOutput, calls=%fused_computation.3 | convolution fusion | flops 4157536 | bytes 401488 | tf_op jit(solution)/shard_map/emt,emd->td/dot_general | solution.py:58
  (5 shorter events, 0.1 us)
Async XLA Ops:
  0.0 1.1 %copy-start = (bf16[4,7168]{1,0:T(4,128)(2,1)S(1)}, bf16[4,7168]{1,0:T(4,128)(2,1)}, u32[]{:S(2)}) copy-start(bf16[4,7168]{1,0:T(4,128)(2,1)} %param.6) | copy-start | bytes 172036
  29.8 23.9 %copy-start.3 = (u32[32]{0:T(128)S(1)}, u32[32]{0:T(128)}, u32[]{:S(2)}) copy-start(u32[32]{0:T(128)} %constant.20) | copy-start | bytes 388
  29.8 25.1 %copy-start.2 = (s32[4,2]{0,1:T(2,128)S(1)}, s32[4,2]{0,1:T(2,128)}, u32[]{:S(2)}) copy-start(s32[4,2]{0,1:T(2,128)} %param.8) | copy-start | bytes 100
  29.8 31.7 %copy-start.1 = (s32[4,2]{0,1:T(2,128)S(1)}, s32[4,2]{0,1:T(2,128)}, u32[]{:S(2)}) copy-start(s32[4,2]{0,1:T(2,128)} %param.7) | copy-start | bytes 100
  49.2 7.3 %collective-permute-start = (bf16[12,7168]{1,0:T(8,128)(2,1)S(1)}, bf16[12,7168]{1,0:T(8,128)(2,1)S(1)}, u32[]{:S(2)}, u32[]{:S(2)}) collective-permute-start(bf16[12,7168]{1,0:T(8,128)(2,1)S(1)} %slice), channel_id=1, source_target_pairs={{0,1},{1,2},{2,3},{4,5},{5,6},{6,7},{8,9},{9,10},{10,11},{12,13},{... | collective-permute-start | bytes 516104
  58.1 9.9 %all-to-all-start.1 = ((bf16[4,3,7168]{2,1,0:T(4,128)(2,1)}), bf16[4,3,7168]{2,1,0:T(4,128)(2,1)S(1)}, u32[]{:S(2)}, u32[]{:S(2)}) async-start(bf16[4,3,7168]{2,1,0:T(4,128)(2,1)} %convert_element_type.45), calls=%async_computation.1 | async-start | bytes 458752 | tf_op jit(solution)/shard_map/all_to_all | solution.py:44
where the time goes:
time: 69.8 us; the launch traced here: 69.4 us
  blocking collectives  34.9 us (50%)
  matrix products  13.9 us (20%)
  waiting for transfers between devices  7.99 us (11%)
  starting transfers between devices  7.75 us (11%)
  local copies, waits for them, and re-layouts  2.9 us (4%)
  other arithmetic  1.12 us (2%)
  between operations  0.79 us (1%)
    all_gather x1, blocking collectives, per_device(): segment = lax.all_gather(slot_flat, 'tok', axis=0, tiled=True)  12.1 us
    unnamed x1, blocking collectives  11.4 us
    all_to_all x1, blocking collectives, per_device(): lax.all_to_all(outgoing, 'ep', split_axis=0, concat_axis=0, tiled=True)  11.4 us
    dot_general x1, matrix products, per_device(): jnp.dot(segment, down_slice, preferred_element_type=jnp.float32)  7.91 us
    all_to_all x1, waiting for transfers between devices, per_device(): lax.all_to_all(summed.reshape(columns, capacity, model_width).astype(jnp....  6.33 us
    dot_general x1, matrix products, per_device(): gate = jnp.dot(segment, gate_slice, preferred_element_type=jnp.float32)  4.43 us
    unnamed x1, starting transfers between devices  4.37 us
    all_to_all x1, starting transfers between devices, per_device(): lax.all_to_all(summed.reshape(columns, capacity, model_width).astype(jnp....  3.38 us
  transfers between devices with their start and end apart: 2, of which 2 were waited for; matrix products, arithmetic and copies ran while one was open for 1% of the time, Pallas kernels for 0%

commit v1 on v0

v1 whole, which is shorter than its diff:
```python
import functools

import jax
import jax.numpy as jnp
from jax import lax
from jax.experimental import pallas as pl
from jax.experimental.pallas import tpu as pltpu
from jax.sharding import PartitionSpec as P

MESH = pl.DeviceIdType.MESH
F32 = jnp.float32
BF16 = jnp.bfloat16


def chunks_of(width, wanted):
    for count in range(wanted, 0, -1):
        if width % (count * 128) == 0:
            return count
    return 1


def kernel(ep, cols, nk, nc, ids_ref, fixed_ref, tok_ref, wg_ref, wu_ref, wd_ref, out_ref,
           wg, wu, wd, tokbuf, wtbuf, xs, gacc, uacc, hid, part, r1, s1, r2, b3, r3,
           wg_sem, wu_sem, wd_sem, own_sem, sz, rz, sx, rx, sc, rc, s1s, r1s, s2s, r2s, s3s, r3s):
    e = lax.axis_index("ep")
    t = lax.axis_index("tok")
    x, c = t // 2, t % 2
    q = c * cols + x
    rows = tok_ref.shape[0]
    kc, nw = tokbuf.shape[-1], part.shape[-1]
    half = part.shape[1] // 2
    block = half // cols

    own = [pltpu.make_async_copy(tok_ref.at[:, pl.ds(k * kc, kc)], tokbuf.at[k, q, e], own_sem.at[k]) for k in range(nk)]
    for cp in own:
        cp.start()
    gcp = [pltpu.make_async_copy(wg_ref.at[0, pl.ds(k * kc, kc), :], wg.at[k], wg_sem.at[k]) for k in range(nk)]
    ucp = [pltpu.make_async_copy(wu_ref.at[0, pl.ds(k * kc, kc), :], wu.at[k], wu_sem.at[k]) for k in range(nk)]
    dcp = [pltpu.make_async_copy(wd_ref.at[0, :, pl.ds(n * nw, nw)], wd.at[n], wd_sem.at[n]) for n in range(nc)]
    for k in range(nk):
        gcp[k].start()
        ucp[k].start()
    for n in range(nc):
        dcp[n].start()

    scores = fixed_ref[...].astype(F32)
    weights = 2.5 * scores / jnp.sum(scores, axis=1, keepdims=True)
    ids = ids_ref[...]
    lane = lax.broadcasted_iota(jnp.int32, (rows, 128), 1)
    table = jnp.zeros((rows, 128), F32)
    for j in range(ids.shape[1]):
        table = table + jnp.where(lane == ids[:, j:j + 1], weights[:, j:j + 1], 0.0)
    wtbuf[q, e] = table

    def at_z(d):
        return {"ep": lax.rem(e + d, ep)}

    def at_x(d):
        return {"tok": lax.rem(x + d, cols) * 2 + c}

    partner = {"tok": x * 2 + 1 - c}
    barrier = pltpu.get_barrier_semaphore()
    for d in range(1, ep):
        pl.semaphore_signal(barrier, inc=1, device_id=at_z(d), device_id_type=MESH)
    for d in range(1, cols):
        pl.semaphore_signal(barrier, inc=1, device_id=at_x(d), device_id_type=MESH)
    pl.semaphore_signal(barrier, inc=1, device_id=partner, device_id_type=MESH)
    pl.semaphore_wait(barrier, ep - 1 + cols - 1 + 1)

    sends = []

    def send(src, dst, ssem, rsem, to):
        cp = pltpu.make_async_remote_copy(src_ref=src, dst_ref=dst, send_sem=ssem, recv_sem=rsem, device_id=to, device_id_type=MESH)
        cp.start()
        sends.append(cp)

    def took(ref, sem):
        pltpu.make_async_copy(ref, ref, sem).wait()

    def buf(k):
        return tokbuf.at[k] if k < nk else wtbuf

    def forward_x(k, d_src, src):
        b = buf(k).at[q, src]
        for d in range(1, cols):
            send(b, b, sx.at[k, d_src, d - 1], rx.at[k, d - 1], at_x(d))

    def begin(k):
        if k < nk:
            own[k].wait()
        b = buf(k).at[q, e]
        for d in range(1, ep):
            send(b, b, sz.at[k, d - 1], rz.at[k, d - 1], at_z(d))
        forward_x(k, 0, e)

    def z_stage(k):
        for d in range(1, ep):
            src = lax.rem(e + ep - d, ep)
            took(buf(k).at[q, src], rz.at[k, d - 1])
            forward_x(k, d, src)
        b = buf(k).at[q]
        send(b, b, sc.at[k, 0], rc.at[k], partner)

    def x_stage(k):
        for d in range(1, cols):
            p = c * cols + lax.rem(x + cols - d, cols)
            b = buf(k).at[p]
            took(b, rx.at[k, d - 1])
            send(b, b, sc.at[k, d], rc.at[k], partner)

    def c_stage(k):
        took(buf(k).at[pl.ds((1 - c) * cols, cols)], rc.at[k])

    group = max(1, 16 // rows)

    def matmuls(k):
        for p in range(2 * cols):
            for g in range(0, ep, group):
                span = min(group, ep - g)
                piece = jnp.concatenate([tokbuf[k, p, g + i].astype(F32) for i in range(span)], axis=0).astype(BF16)
                xs[pl.ds((p * ep + g) * rows, span * rows), :] = piece
        gcp[k].wait()
        gate = jnp.dot(xs[...], wg[k], preferred_element_type=F32)
        if k == 0:
            gacc[...] = gate
        else:
            gacc[...] += gate
        ucp[k].wait()
        up = jnp.dot(xs[...], wu[k], preferred_element_type=F32)
        if k == 0:
            uacc[...] = up
        else:
            uacc[...] += up

    order = list(range(nk))
    for k in range(nk + 1):
        begin(k)
    for s in range(nk + 3):
        if s <= nk:
            z_stage(s)
        if 0 <= s - 1 <= nk:
            x_stage(s - 1)
        if 0 <= s - 2 <= nk:
            c_stage(s - 2)
            if s - 2 < nk:
                matmuls(s - 2)

    tab = jnp.concatenate([wtbuf[p, i] for p in range(2 * cols) for i in range(ep)], axis=0)
    lanes = lax.broadcasted_iota(jnp.int32, tab.shape, 1)
    scale = jnp.sum(jnp.where(lanes == e, tab, 0.0), axis=1, keepdims=True)
    gate = gacc[...]
    hid[...] = (gate / (1.0 + jnp.exp(-gate)) * uacc[...] * scale).astype(BF16)

    def down(n):
        dcp[n].wait()
        part[n] = jnp.dot(hid[...], wd[n], preferred_element_type=F32).astype(BF16)
        send(part.at[n, pl.ds((1 - c) * half, half)], r1.at[n], s1s.at[n], r1s.at[n], partner)

    def sum_core(n):
        took(r1.at[n], r1s.at[n])
        mine = part[n, pl.ds(c * half, half), :].astype(F32) + r1[n].astype(F32)
        s1[n] = mine.astype(BF16)
        for d in range(1, cols):
            to = lax.rem(x + d, cols)
            send(s1.at[n, pl.ds(to * block, block)], r2.at[n, d - 1], s2s.at[n, d - 1], r2s.at[n], at_x(d))

    def sum_x(n):
        took(r2.at[n], r2s.at[n])
        mine = s1[n, pl.ds(x * block, block), :].astype(F32)
        for d in range(cols - 1):
            mine = mine + r2[n, d].astype(F32)
        for i in range(ep):
            b3[n, i] = mine[i * rows:(i + 1) * rows].astype(BF16)
        for d in range(1, ep):
            to = lax.rem(e + d, ep)
            send(b3.at[n, to], r3.at[n, d - 1], s3s.at[n, d - 1], r3s.at[n], at_z(d))

    def sum_z(n):
        took(r3.at[n], r3s.at[n])
        total = b3[n, e].astype(F32)
        for d in range(ep - 1):
            total = total + r3[n, d].astype(F32)
        out_ref[:, n * nw:(n + 1) * nw] = total.astype(BF16)

    for s in range(nc + 3):
        if s < nc:
            down(s)
        if 0 <= s - 1 < nc:
            sum_core(s - 1)
        if 0 <= s - 2 < nc:
            sum_x(s - 2)
        if 0 <= s - 3 < nc:
            sum_z(s - 3)
    for cp in sends:
        cp.wait_send()


def solution(mesh):
    ep, tok = mesh.shape["ep"], mesh.shape["tok"]
    cols = tok // 2

    def step(tokens, expert_ids, gate_fixed, w_gate, w_up, w_down):
        rows, width = tokens.shape
        ff = w_gate.shape[2]
        m = ep * tok * rows
        nk = chunks_of(width, 4)
        nc = chunks_of(width, 4)
        kc, nw = width // nk, width // nc
        dma = pltpu.SemaphoreType.DMA
        vmem = pl.BlockSpec(memory_space=pltpu.VMEM)
        anywhere = pl.BlockSpec(memory_space=pl.ANY)
        return pl.pallas_call(
            functools.partial(kernel, ep, cols, nk, nc),
            out_shape=jax.ShapeDtypeStruct((rows, width), BF16),
            in_specs=[vmem, vmem, anywhere, anywhere, anywhere, anywhere],
            out_specs=vmem,
            scratch_shapes=[
                pltpu.VMEM((nk, kc, ff), BF16),
                pltpu.VMEM((nk, kc, ff), BF16),
                pltpu.VMEM((nc, ff, nw), BF16),
                pltpu.VMEM((nk, tok, ep, rows, kc), BF16),
                pltpu.VMEM((tok, ep, rows, 128), F32),
                pltpu.VMEM((m, kc), BF16),
                pltpu.VMEM((m, ff), F32),
                pltpu.VMEM((m, ff), F32),
                pltpu.VMEM((m, ff), BF16),
                pltpu.VMEM((nc, m, nw), BF16),
                pltpu.VMEM((nc, m // 2, nw), BF16),
                pltpu.VMEM((nc, m // 2, nw), BF16),
                pltpu.VMEM((nc, cols - 1, ep * rows, nw), BF16),
                pltpu.VMEM((nc, ep, rows, nw), BF16),
                pltpu.VMEM((nc, ep - 1, rows, nw), BF16),
                dma((nk,)), dma((nk,)), dma((nc,)), dma((nk,)),
                dma((nk + 1, ep - 1)), dma((nk + 1, ep - 1)),
                dma((nk + 1, ep, cols - 1)), dma((nk + 1, cols - 1)),
                dma((nk + 1, cols)), dma((nk + 1,)),
                dma((nc,)), dma((nc,)),
                dma((nc, cols - 1)), dma((nc,)),
                dma((nc, ep - 1)), dma((nc,)),
            ],
            compiler_params=pltpu.CompilerParams(
                collective_id=0, has_side_effects=True, vmem_limit_bytes=64000000,
            ),
        )(expert_ids, gate_fixed, tokens, w_gate, w_up, w_down)

    rows_spec = P(("groups", "ep", "tok"), None)
    return jax.shard_map(
        step, mesh=mesh,
        in_specs=(rows_spec, rows_spec, rows_spec, P("ep", None, "tok"), P("ep", None, "tok"), P("ep", "tok", None)),
        out_specs=rows_spec, check_vma=False,
    )
```

time: 69.8 us -> 42.1 us (0.60)
  the two profiles are of different devices: /device:TPU:1 before, /device:TPU:0 now
where the time goes in v1:
time: 42.1 us; the launch traced here: 41.9 us
  Pallas kernels  37.7 us (90%)
  local copies, waits for them, and re-layouts  4.12 us (10%)
    pallas_call x1, Pallas kernels, step(): pl.pallas_call(functools.partial(kernel, ep, cols, nk, nc), out_shape=jax...  37.7 us
    unnamed x3, local copies, waits for them, and re-layouts  4.12 us

profile of v1, /device:TPU:0, one launch (start us, length us, event | category | flops | bytes accessed | tf_op | source)
XLA Modules:
  0.0 41.9 jit_solution(16631368936169915850)
XLA Ops:
  0.0 1.3 %copy.7.ids_ref = s32[4,2]{1,0:T(4,128)} copy(s32[4,2]{0,1:T(2,128)} %param.7) | data formatting | bytes 64 | tf_op args[1]
  1.3 1.3 %copy.8.fixed_ref = s32[4,2]{1,0:T(4,128)} copy(s32[4,2]{0,1:T(2,128)} %param.8) | data formatting | bytes 64 | tf_op args[2]
  2.7 37.7 %shard_map.64 = bf16[4,7168]{1,0:T(4,128)(2,1)} custom-call(s32[4,2]{1,0:T(4,128)} %copy.7.ids_ref, s32[4,2]{1,0:T(4,128)} %copy.8.fixed_ref, bf16[4,7168]{1,0:T(4,128)(2,1)} %tok_ref.1, bf16[1,7168,512]{2,1,0:T(8,128)(2,1)} %wg_ref.1, bf16[1,7168,512]{2,1,0:T(8,128)(2,1)} %wu_ref.1, bf16[1,512,7168]{2,1,0:T(8,128)(2,1)} %wd_ref.1), custom_call_target="tpu_custom_call" | custom-call | tf_op jit(solution)/shard_map/pallas_call | solution.py:212
  40.4 1.5 %copy.10 = bf16[4,7168]{1,0:T(4,128)(2,1)} copy(bf16[4,7168]{1,0:T(4,128)(2,1)} %shard_map.64) | data formatting | bytes 114688

commit v2 on v1

--- a/solution.py
+++ b/solution.py
@@ -10,6 +10,9 @@
 MESH = pl.DeviceIdType.MESH
 F32 = jnp.float32
 BF16 = jnp.bfloat16
+NK, NC = 2, 4
+AGX, AGC = 1, 1
+LAG1, LAG2, LAG3 = 1, 3, 3
 
 
 def chunks_of(width, wanted):
@@ -19,9 +22,18 @@
     return 1
 
 
-def kernel(ep, cols, nk, nc, ids_ref, fixed_ref, tok_ref, wg_ref, wu_ref, wd_ref, out_ref,
-           wg, wu, wd, tokbuf, wtbuf, xs, gacc, uacc, hid, part, r1, s1, r2, b3, r3,
-           wg_sem, wu_sem, wd_sem, own_sem, sz, rz, sx, rx, sc, rc, s1s, r1s, s2s, r2s, s3s, r3s):
+def paired(v, d):
+    bit = 1
+    while bit <= d:
+        if d & bit:
+            v = v + bit - 2 * bit * (lax.rem(v // bit, 2))
+        bit *= 2
+    return v
+
+
+def kernel(ep, cols, nk, nc, ids_hbm, fixed_hbm, tok_ref, wg_ref, wu_ref, wd_ref, out_ref,
+           ids_ref, fixed_ref, wg, wu, wd, tokbuf, wtbuf, xs, gacc, uacc, hid, part, r1, s1, r2, b3, r3,
+           id_sem, wg_sem, wu_sem, wd_sem, own_sem, sz, rz, sx, rx, sc, rc, s1s, r1s, s2s, r2s, s3s, r3s):
     e = lax.axis_index("ep")
     t = lax.axis_index("tok")
     x, c = t // 2, t % 2
@@ -31,6 +43,9 @@
     half = part.shape[1] // 2
     block = half // cols
 
+    idcp = [pltpu.make_async_copy(a, b, id_sem.at[i]) for i, (a, b) in enumerate(((ids_hbm, ids_ref), (fixed_hbm, fixed_ref)))]
+    for cp in idcp:
+        cp.start()
     own = [pltpu.make_async_copy(tok_ref.at[:, pl.ds(k * kc, kc)], tokbuf.at[k, q, e], own_sem.at[k]) for k in range(nk)]
     for cp in own:
         cp.start()
@@ -43,17 +58,8 @@
     for n in range(nc):
         dcp[n].start()
 
-    scores = fixed_ref[...].astype(F32)
-    weights = 2.5 * scores / jnp.sum(scores, axis=1, keepdims=True)
-    ids = ids_ref[...]
-    lane = lax.broadcasted_iota(jnp.int32, (rows, 128), 1)
-    table = jnp.zeros((rows, 128), F32)
-    for j in range(ids.shape[1]):
-        table = table + jnp.where(lane == ids[:, j:j + 1], weights[:, j:j + 1], 0.0)
-    wtbuf[q, e] = table
-
     def at_z(d):
-        return {"ep": lax.rem(e + d, ep)}
+        return {"ep": paired(e, d)}
 
     def at_x(d):
         return {"tok": lax.rem(x + d, cols) * 2 + c}
@@ -65,6 +71,21 @@
     for d in range(1, cols):
         pl.semaphore_signal(barrier, inc=1, device_id=at_x(d), device_id_type=MESH)
     pl.semaphore_signal(barrier, inc=1, device_id=partner, device_id_type=MESH)
+    for cp in idcp:
+        cp.wait()
+    scores = fixed_ref[...].astype(F32)
+    weights = 2.5 * scores / jnp.sum(scores, axis=0, keepdims=True)
+    ids = ids_ref[...].astype(F32)
+    lane = lax.broadcasted_iota(jnp.int32, (rows, 128), 1).astype(F32)
+    eye = lax.broadcasted_iota(jnp.int32, (rows, rows), 0) == lax.broadcasted_iota(jnp.int32, (rows, rows), 1)
+
+    def column(row):
+        return jnp.sum(jnp.where(eye, jnp.broadcast_to(row, (rows, rows)), 0.0), axis=1, keepdims=True)
+
+    table = jnp.zeros((rows, 128), F32)
+    for j in range(ids.shape[0]):
+        table = table + jnp.where(lane == column(ids[j:j + 1]), column(weights[j:j + 1]), 0.0)
+    wtbuf[q, e] = table
     pl.semaphore_wait(barrier, ep - 1 + cols - 1 + 1)
 
     sends = []
@@ -95,7 +116,7 @@
 
     def z_stage(k):
         for d in range(1, ep):
-            src = lax.rem(e + ep - d, ep)
+            src = paired(e, d)
             took(buf(k).at[q, src], rz.at[k, d - 1])
             forward_x(k, d, src)
         b = buf(k).at[q]
@@ -132,18 +153,17 @@
         else:
             uacc[...] += up
 
-    order = list(range(nk))
     for k in range(nk + 1):
         begin(k)
-    for s in range(nk + 3):
+    for s in range(nk + 1 + AGX + AGC):
         if s <= nk:
             z_stage(s)
-        if 0 <= s - 1 <= nk:
-            x_stage(s - 1)
-        if 0 <= s - 2 <= nk:
-            c_stage(s - 2)
-            if s - 2 < nk:
-                matmuls(s - 2)
+        if 0 <= s - AGX <= nk:
+            x_stage(s - AGX)
+        if 0 <= s - AGX - AGC <= nk:
+            c_stage(s - AGX - AGC)
+            if s - AGX - AGC < nk:
+                matmuls(s - AGX - AGC)
 
     tab = jnp.concatenate([wtbuf[p, i] for p in range(2 * cols) for i in range(ep)], axis=0)
     lanes = lax.broadcasted_iota(jnp.int32, tab.shape, 1)
@@ -172,7 +192,7 @@
         for i in range(ep):
             b3[n, i] = mine[i * rows:(i + 1) * rows].astype(BF16)
         for d in range(1, ep):
-            to = lax.rem(e + d, ep)
+            to = paired(e, d)
             send(b3.at[n, to], r3.at[n, d - 1], s3s.at[n, d - 1], r3s.at[n], at_z(d))
 
     def sum_z(n):
@@ -182,15 +202,15 @@
             total = total + r3[n, d].astype(F32)
         out_ref[:, n * nw:(n + 1) * nw] = total.astype(BF16)
 
-    for s in range(nc + 3):
+    for s in range(nc + LAG1 + LAG2 + LAG3):
         if s < nc:
             down(s)
-        if 0 <= s - 1 < nc:
-            sum_core(s - 1)
-        if 0 <= s - 2 < nc:
-            sum_x(s - 2)
-        if 0 <= s - 3 < nc:
-            sum_z(s - 3)
+        if 0 <= s - LAG1 < nc:
+            sum_core(s - LAG1)
+        if 0 <= s - LAG1 - LAG2 < nc:
+            sum_x(s - LAG1 - LAG2)
+        if 0 <= s - LAG1 - LAG2 - LAG3 < nc:
+            sum_z(s - LAG1 - LAG2 - LAG3)
     for cp in sends:
         cp.wait_send()
 
@@ -203,8 +223,8 @@
         rows, width = tokens.shape
         ff = w_gate.shape[2]
         m = ep * tok * rows
-        nk = chunks_of(width, 4)
-        nc = chunks_of(width, 4)
+        nk = chunks_of(width, NK)
+        nc = chunks_of(width, NC)
         kc, nw = width // nk, width // nc
         dma = pltpu.SemaphoreType.DMA
         vmem = pl.BlockSpec(memory_space=pltpu.VMEM)
@@ -212,9 +232,11 @@
         return pl.pallas_call(
             functools.partial(kernel, ep, cols, nk, nc),
             out_shape=jax.ShapeDtypeStruct((rows, width), BF16),
-            in_specs=[vmem, vmem, anywhere, anywhere, anywhere, anywhere],
+            in_specs=[anywhere, anywhere, anywhere, anywhere, anywhere, anywhere],
             out_specs=vmem,
             scratch_shapes=[
+                pltpu.VMEM(expert_ids.shape[::-1], jnp.int32),
+                pltpu.VMEM(gate_fixed.shape[::-1], jnp.int32),
                 pltpu.VMEM((nk, kc, ff), BF16),
                 pltpu.VMEM((nk, kc, ff), BF16),
                 pltpu.VMEM((nc, ff, nw), BF16),
@@ -230,7 +252,7 @@
                 pltpu.VMEM((nc, cols - 1, ep * rows, nw), BF16),
                 pltpu.VMEM((nc, ep, rows, nw), BF16),
                 pltpu.VMEM((nc, ep - 1, rows, nw), BF16),
-                dma((nk,)), dma((nk,)), dma((nc,)), dma((nk,)),
+                dma((2,)), dma((nk,)), dma((nk,)), dma((nc,)), dma((nk,)),
                 dma((nk + 1, ep - 1)), dma((nk + 1, ep - 1)),
                 dma((nk + 1, ep, cols - 1)), dma((nk + 1, cols - 1)),
                 dma((nk + 1, cols)), dma((nk + 1,)),
@@ -241,7 +263,7 @@
             compiler_params=pltpu.CompilerParams(
                 collective_id=0, has_side_effects=True, vmem_limit_bytes=64000000,
             ),
-        )(expert_ids, gate_fixed, tokens, w_gate, w_up, w_down)
+        )(expert_ids.T, gate_fixed.T, tokens, w_gate, w_up, w_down)
 
     rows_spec = P(("groups", "ep", "tok"), None)
     return jax.shard_map(

time: 42.1 us -> 35.1 us (0.83)
  Pallas kernels: 37.7 us -> 33.5 us
  local copies, waits for them, and re-layouts: 4.12 us -> 1.46 us
    pallas_call x1, Pallas kernels: 37.7 us -> 33.5 us  [step(): pl.pallas_call(functools.partial(kernel, ep, cols, nk, nc), out_shape=jax...]
    unnamed x3 -> x1, local copies, waits for them, and re-layouts: 4.12 us -> 1.46 us
where the time goes in v2:
time: 35.1 us; the launch traced here: 35 us
  Pallas kernels  33.5 us (95%)
  local copies, waits for them, and re-layouts  1.46 us (4%)
    pallas_call x1, Pallas kernels, step(): pl.pallas_call(functools.partial(kernel, ep, cols, nk, nc), out_shape=jax...  33.5 us
    unnamed x1, local copies, waits for them, and re-layouts  1.46 us

profile of v2, /device:TPU:0, one launch (start us, length us, event | category | flops | bytes accessed | tf_op | source)
XLA Modules:
  0.0 35.0 jit_solution(2348929944764762395)
XLA Ops:
  0.0 33.5 %shard_map.64 = bf16[4,7168]{1,0:T(4,128)(2,1)} custom-call(s32[2,4]{1,0:T(2,128)} %bitcast.2, s32[2,4]{1,0:T(2,128)} %bitcast.3, bf16[4,7168]{1,0:T(4,128)(2,1)} %tok_ref.1, bf16[1,7168,512]{2,1,0:T(8,128)(2,1)} %wg_ref.1, bf16[1,7168,512]{2,1,0:T(8,128)(2,1)} %wu_ref.1, bf16[1,512,7168]{2,1,0:T(8,128)(2,1)} %wd_ref.1), custom_call_target="tpu_custom_call" | custom-call | tf_op jit(solution)/shard_map/pallas_call | solution.py:232
  33.5 1.5 %copy.8 = bf16[4,7168]{1,0:T(4,128)(2,1)} copy(bf16[4,7168]{1,0:T(4,128)(2,1)} %shard_map.64) | data formatting | bytes 114688

commit v3 on v2

--- a/solution.py
+++ b/solution.py
@@ -11,7 +11,7 @@
 F32 = jnp.float32
 BF16 = jnp.bfloat16
 NK, NC = 2, 4
-AGX, AGC = 1, 1
+AGX, AGC = 2, 1
 LAG1, LAG2, LAG3 = 1, 3, 3
 
 
@@ -135,11 +135,14 @@
     group = max(1, 16 // rows)
 
     def matmuls(k):
-        for p in range(2 * cols):
+        for i_p in range(2 * cols):
+            if i_p == cols:
+                c_stage(k)
+            p = (c if i_p < cols else 1 - c) * cols + i_p % cols
             for g in range(0, ep, group):
                 span = min(group, ep - g)
                 piece = jnp.concatenate([tokbuf[k, p, g + i].astype(F32) for i in range(span)], axis=0).astype(BF16)
-                xs[pl.ds((p * ep + g) * rows, span * rows), :] = piece
+                xs[pl.ds(pl.multiple_of((p * ep + g) * rows, span * rows), span * rows), :] = piece
         gcp[k].wait()
         gate = jnp.dot(xs[...], wg[k], preferred_element_type=F32)
         if k == 0:
@@ -161,9 +164,10 @@
         if 0 <= s - AGX <= nk:
             x_stage(s - AGX)
         if 0 <= s - AGX - AGC <= nk:
-            c_stage(s - AGX - AGC)
             if s - AGX - AGC < nk:
                 matmuls(s - AGX - AGC)
+            else:
+                c_stage(nk)
 
     tab = jnp.concatenate([wtbuf[p, i] for p in range(2 * cols) for i in range(ep)], axis=0)
     lanes = lax.broadcasted_iota(jnp.int32, tab.shape, 1)

time: 35.1 us -> 34.8 us (level)
  no operation moved by 1% of the time
where the time goes in v3:
time: 34.8 us; the launch traced here: 34.7 us
  Pallas kernels  33.2 us (95%)
  local copies, waits for them, and re-layouts  1.46 us (4%)
    pallas_call x1, Pallas kernels, step(): pl.pallas_call(functools.partial(kernel, ep, cols, nk, nc), out_shape=jax...  33.2 us
    unnamed x1, local copies, waits for them, and re-layouts  1.46 us

profile of v3, /device:TPU:0, one launch (start us, length us, event | category | flops | bytes accessed | tf_op | source)
XLA Modules:
  0.0 34.7 jit_solution(6862538260435552401)
XLA Ops:
  0.0 33.2 %shard_map.64 = bf16[4,7168]{1,0:T(4,128)(2,1)} custom-call(s32[2,4]{1,0:T(2,128)} %bitcast.2, s32[2,4]{1,0:T(2,128)} %bitcast.3, bf16[4,7168]{1,0:T(4,128)(2,1)} %tok_ref.1, bf16[1,7168,512]{2,1,0:T(8,128)(2,1)} %wg_ref.1, bf16[1,7168,512]{2,1,0:T(8,128)(2,1)} %wu_ref.1, bf16[1,512,7168]{2,1,0:T(8,128)(2,1)} %wd_ref.1), custom_call_target="tpu_custom_call" | custom-call | tf_op jit(solution)/shard_map/pallas_call | solution.py:236
  33.2 1.5 %copy.8 = bf16[4,7168]{1,0:T(4,128)(2,1)} copy(bf16[4,7168]{1,0:T(4,128)(2,1)} %shard_map.64) | data formatting | bytes 114688
